TPU v7x, 32 devices: a whole 2x2x4 slice. The times are simulated.
32 devices in a mesh: grp: 2 (over y), kvp: 4 (over x, core), tp: 4 (over z).
Axes of the slice: x: 2, y: 2, z: 4, core: 2. Of those that a mesh axis runs over, the one named last changes fastest.
Arguments:
- hidden_in: bfloat16 [16, 7168], P('grp'), parts along dimension 0, may hold values from -3 to 3
- queries_nope: bfloat16 [16, 128, 128], P('grp', ('kvp', 'tp')), parts along dimension 0, may hold values from -6 to 6
- queries_rope: bfloat16 [16, 128, 64], P('grp', ('kvp', 'tp')), parts along dimension 0, may hold values from -26 to 26
- cache: bfloat16 [16, 1536, 576], P('grp', 'kvp'), parts along dimension 0, may hold values from -20 to 20
- lengths: int32 [16], P('grp'), parts along dimension 0, may hold values from 128 to 1536, as said below
- w_uk: bfloat16 [128, 128, 512], P(('kvp', 'tp')), may hold values from -0.5 to 0.5
- w_uv: bfloat16 [128, 512, 128], P(('kvp', 'tp')), may hold values from -0.25 to 0.25
- w_out: bfloat16 [16384, 7168], P(('kvp', 'tp')), may hold values from -0.0625 to 0.0625
- norm_gain: float32 [7168], replicated, may hold values from 0.25 to 1.75
- w_gate: bfloat16 [7168, 18432], P(None, ('kvp', 'tp')), may hold values from -0.0625 to 0.0625
- w_up: bfloat16 [7168, 18432], P(None, ('kvp', 'tp')), may hold values from -0.0625 to 0.0625
- w_down: bfloat16 [18432, 7168], P(('kvp', 'tp')), may hold values from -0.0625 to 0.0625
Outputs:
- layer_out: bfloat16 [16, 7168], P('grp', ('kvp', 'tp')), parts along dimension 0
There are 2 independent parts, one for each index of `grp`. A program takes and returns all parts, laid end to end along the dimension named above; an argument that names none is the same for every part. Nothing has to cross between parts.
Inputs may be any that keep to these rules, and one draw needn't show every extreme that they name: `lengths`: every length is a multiple of 128; in every draw some request has the full 1536.
All inputs are finite; a program needn't handle non-finite values.
Results may differ from a plain program's by a relative error of at most 0.04.
Values may be sent and summed in bfloat16 or wider, within the bound.
A program may use at most 128 MiB of HBM per device.

v0:
```python
import jax
import jax.numpy as jnp
from jax import lax
from jax.sharding import PartitionSpec as P


def project(o_lat, w_uv, w_out):
    head_out = jnp.einsum("bhl,hle->bhe", o_lat, w_uv, preferred_element_type=jnp.float32).astype(
        jnp.bfloat16
    )
    return jnp.dot(
        head_out.reshape(head_out.shape[0], -1), w_out, preferred_element_type=jnp.float32
    )


def per_device(
    hidden_in,
    queries_nope,
    queries_rope,
    cache,
    lengths,
    w_uk,
    w_uv,
    w_out,
    norm_gain,
    w_gate,
    w_up,
    w_down,
):
    batch, heads_dev, head_dim = queries_nope.shape
    latent = w_uk.shape[2]
    ctx_dev = cache.shape[1]
    groups = lax.axis_size("kvp")
    score_scale = float(head_dim + queries_rope.shape[2]) ** (-0.5)
    q_lat = jnp.einsum(
        "bhd,hdl->bhl", queries_nope, w_uk, preferred_element_type=jnp.float32
    ).astype(jnp.bfloat16)
    q_lat_all, rope_all = (
        lax.all_gather(q_lat, "kvp", axis=1, tiled=True),
        lax.all_gather(queries_rope, "kvp", axis=1, tiled=True),
    )
    q_full = jnp.concatenate([q_lat_all, rope_all], axis=2)
    scores = (
        jnp.einsum("bhc,btc->bht", q_full, cache, preferred_element_type=jnp.float32) * score_scale
    )
    offset = lax.axis_index("kvp") * ctx_dev
    visible = ((offset + jnp.arange(ctx_dev, dtype=jnp.int32))[None, :] < lengths[:, None])[
        :, None, :
    ]
    masked = jnp.where(visible, scores, jnp.float32(-1e30))
    block_max = jnp.max(masked, axis=2)
    exponent = jnp.where(visible, jnp.exp(masked - block_max[..., None]), jnp.float32(0.0))
    guarded = jnp.maximum(jnp.sum(exponent, axis=2), 1.0)
    log_total = block_max + jnp.log(guarded)
    weights = (exponent / guarded[..., None]).astype(jnp.bfloat16)
    partial_value = jnp.einsum("bht,btc->bhc", weights, cache, preferred_element_type=jnp.float32)[
        ..., :latent
    ]
    blocks = partial_value.reshape(batch, groups, heads_dev, latent)
    block_logs = log_total.reshape(batch, groups, heads_dev)
    part_blocks = lax.all_to_all(
        blocks.astype(jnp.bfloat16), "kvp", split_axis=1, concat_axis=1, tiled=True
    ).astype(blocks.dtype)
    part_logs = lax.all_to_all(
        block_logs.astype(jnp.bfloat16), "kvp", split_axis=1, concat_axis=1, tiled=True
    ).astype(block_logs.dtype)
    highest = jnp.max(part_logs, axis=1)
    overall = highest + jnp.log(jnp.sum(jnp.exp(part_logs - highest[:, None, :]), axis=1))
    scaled = jnp.exp(part_logs - overall[:, None, :])[..., None] * part_blocks
    o_lat = jnp.sum(scaled, axis=1).astype(jnp.bfloat16)
    attention = project(o_lat, w_uv, w_out)
    model_width = norm_gain.shape[0]
    share_width = model_width // lax.axis_size(("kvp", "tp"))
    share_start = lax.axis_index(("kvp", "tp")) * share_width
    attn_whole = lax.psum(attention, ("kvp", "tp"))
    residual = hidden_in.astype(jnp.float32) + attn_whole
    mean_square = jnp.mean(residual * residual, axis=1)
    normed = (residual * lax.rsqrt(mean_square + 1e-06)[:, None] * norm_gain[None, :]).astype(
        jnp.bfloat16
    )
    residual_share = lax.dynamic_slice_in_dim(residual, share_start, share_width, 1)
    gate_proj = jnp.dot(normed, w_gate, preferred_element_type=jnp.float32)
    up_proj = jnp.dot(normed, w_up, preferred_element_type=jnp.float32)
    act = (jax.nn.silu(gate_proj) * up_proj).astype(jnp.bfloat16)
    ffn_terms = jnp.dot(act, w_down, preferred_element_type=jnp.float32)
    ffn_share = lax.psum_scatter(ffn_terms, ("kvp", "tp"), scatter_dimension=1, tiled=True)
    return (residual_share + ffn_share).astype(jnp.bfloat16)


def solution(mesh):
    placed = (
        P("grp", None),
        P("grp", ("kvp", "tp"), None),
        P("grp", ("kvp", "tp"), None),
        P("grp", "kvp", None),
        P("grp"),
        P(("kvp", "tp"), None, None),
        P(("kvp", "tp"), None, None),
        P(("kvp", "tp"), None),
        P(),
        P(None, ("kvp", "tp")),
        P(None, ("kvp", "tp")),
        P(("kvp", "tp"), None),
    )
    return jax.shard_map(
        per_device, mesh=mesh, in_specs=placed, out_specs=P("grp", ("kvp", "tp")), check_vma=False
    )
```

profile of v0, /device:TPU:0, one launch (start us, length us, event | category | flops | bytes accessed | tf_op | source)
XLA Modules:
  0.0 248.7 jit_solution(1045707272200250479)
XLA Ops:
  6.5 0.9 copy.24
  7.4 6.3 %all_gather.7 = bf16[8,32,64]{2,0,1:T(8,128)(2,1)S(1)} all-gather(bf16[8,8,64]{2,0,1:T(8,128)(2,1)S(1)} %copy.24), channel_id=1, replica_groups=mesh['grp'=2,'kvp'=4,'tp'=4] {'kvp'}, dimensions={1}, use_global_device_ids=true | all-gather | bytes 40960 | tf_op jit(solution)/shard_map/all_gather | solution.py:40
  13.7 1.5 fusion.2
  15.2 6.3 %all_gather.6 = bf16[8,32,512]{2,0,1:T(8,128)(2,1)S(1)} all-gather(bf16[8,8,512]{2,0,1:T(8,128)(2,1)S(1)} %fusion.2), channel_id=1, replica_groups=mesh['grp'=2,'kvp'=4,'tp'=4] {'kvp'}, dimensions={1}, use_global_device_ids=true | all-gather | bytes 327680 | tf_op jit(solution)/shard_map/all_gather | solution.py:39
  21.6 0.7 broadcast_compare_fusion
  22.3 0.7 fusion.31
  23.0 0.7 copy-done.3
  24.6 0.8 convert_element_type.50
  25.3 0.6 copy.27
  25.9 3.2 %all-to-all-start = ((bf16[8,4,8]{2,0,1:T(8,128)(2,1)}), bf16[8,4,8]{2,0,1:T(8,128)(2,1)S(1)}, u32[]{:S(2)}, u32[]{:S(2)}) async-start(bf16[8,4,8]{2,0,1:T(8,128)(2,1)} %copy.27), calls=%async_computation | async-start | bytes 16384 | tf_op jit(solution)/shard_map/all_to_all | solution.py:64
  29.2 2.2 fusion.10
  31.5 0.7 copy.28
  32.2 0.8 all-to-all-done
  33.0 3.4 %all-to-all-start.1 = ((bf16[8,4,8,512]{3,2,0,1:T(8,128)(2,1)}), bf16[8,4,8,512]{3,2,0,1:T(8,128)(2,1)S(1)}, u32[]{:S(2)}, u32[]{:S(2)}) async-start(bf16[8,4,8,512]{3,2,0,1:T(8,128)(2,1)} %copy.28), calls=%async_computation.1 | async-start | bytes 524288 | tf_op jit(solution)/shard_map/all_to_all | solution.py:61
  36.5 5.8 %all-to-all-done.1 = bf16[8,4,8,512]{3,2,0,1:T(8,128)(2,1)S(1)} async-done(((bf16[8,4,8,512]{3,2,0,1:T(8,128)(2,1)}), bf16[8,4,8,512]{3,2,0,1:T(8,128)(2,1)S(1)}, u32[]{:S(2)}, u32[]{:S(2)}) %all-to-all-start.1) | async-done | bytes 262176 | tf_op jit(solution)/shard_map/all_to_all | solution.py:61
  42.5 8.4 %fusion.4 = f32[8,7168]{1,0:T(8,128)} fusion(bf16[1024,7168]{1,0:T(8,128)(2,1)} %param.19, bf16[8,512,128]{2,1,0:T(8,128)(2,1)} %param.18, bf16[8,8,512]{2,1,0:T(8,128)(2,1)S(1)} %multiply_reduce_fusion), kind=kOutput, calls=%fused_computation.9 | convolution fusion | flops 125837312 | bytes 16023552 | tf_op jit(solution)/shard_map/dot_general | solution.py:11
  50.9 89.8 %all-reduce.2.cloned.1.call-done = f32[8,7168]{1,0:T(8,128)} async-done(((f32[8,7168]{1,0:T(8,128)}), f32[8,7168]{1,0:T(8,128)}) %all-reduce.2.cloned.1.call-update) | async-done | bytes 229392 | tf_op jit(solution)/shard_map/psum | solution.py:75
  140.7 1.1 multiply_reduce_fusion.1
  141.8 0.7 copy-done.2
  142.5 8.6 %fusion.30 = f32[8,1152]{1,0:T(8,128)} fusion(bf16[7168,1152]{1,0:T(8,128)(2,1)} %param.21, f32[8,7168]{1,0:T(8,128)S(1)} %get-tuple-element.6, f32[7168]{0:T(1024)S(1)} %copy-done.4, f32[8]{0:T(128)S(1)} %add_rsqrt_fusion), kind=kOutput, calls=%fused_computation.50 | convolution fusion | flops 132292608 | bytes 16810016 | tf_op jit(solution)/shard_map/dot_general | solution.py:82
  151.1 18.6 %convolution_bitcast_fusion = f32[7168,8]{1,0:T(8,128)} fusion(bf16[1152,7168]{1,0:T(8,128)(2,1)} %param.23, bf16[7168,1152]{1,0:T(8,128)(2,1)} %param.22, f32[8,1152]{1,0:T(8,128)} %fusion.30, f32[8,7168]{1,0:T(8,128)} %copy-done.2, f32[7168]{0:T(1024)} %param.20, f32[8]{0:T(128)S(1)} %add_rsqrt_fusion), kind=kOutput, calls=%fused_computation | convolution fusion | flops 264468480 | bytes 33554464
  169.7 69.7 %reduce-scatter.4.cloned.1.call-done = f32[448,8]{1,0:T(8,128)} async-done(((f32[7168,8]{1,0:T(8,128)}), f32[448,8]{1,0:T(8,128)}) %reduce-scatter.4.cloned.1.call-update) | async-done | bytes 14352
  239.4 1.0 copy.32
  240.4 1.4 add_convert_fusion
  (27 shorter events, 1.2 us)
Async XLA Ops:
  6.5 15.7 %copy-start = (bf16[8,384,576]{1,2,0:T(8,128)(2,1)S(1)}, bf16[8,384,576]{1,2,0:T(8,128)(2,1)}, u32[]{:S(2)}) copy-start(bf16[8,384,576]{1,2,0:T(8,128)(2,1)} %param.15) | copy-start | bytes 10616836
  23.0 0.7 copy-start.3
  25.9 7.0 %all-to-all-start = ((bf16[8,4,8]{2,0,1:T(8,128)(2,1)}), bf16[8,4,8]{2,0,1:T(8,128)(2,1)S(1)}, u32[]{:S(2)}, u32[]{:S(2)}) async-start(bf16[8,4,8]{2,0,1:T(8,128)(2,1)} %copy.27), calls=%async_computation | async-start | bytes 16384 | tf_op jit(solution)/shard_map/all_to_all | solution.py:64
  31.4 109.2 %copy-start.5 = (bf16[8,7168]{1,0:T(8,128)(2,1)S(1)}, bf16[8,7168]{1,0:T(8,128)(2,1)}, u32[]{:S(2)}) copy-start(bf16[8,7168]{1,0:T(8,128)(2,1)} %param.12) | copy-start | bytes 344068
  31.5 111.0 %copy-start.4 = (f32[7168]{0:T(1024)S(1)}, f32[7168]{0:T(1024)}, u32[]{:S(2)}) copy-start(f32[7168]{0:T(1024)} %param.20) | copy-start | bytes 86020
  33.0 9.4 %all-to-all-start.1 = ((bf16[8,4,8,512]{3,2,0,1:T(8,128)(2,1)}), bf16[8,4,8,512]{3,2,0,1:T(8,128)(2,1)S(1)}, u32[]{:S(2)}, u32[]{:S(2)}) async-start(bf16[8,4,8,512]{3,2,0,1:T(8,128)(2,1)} %copy.28), calls=%async_computation.1 | async-start | bytes 524288 | tf_op jit(solution)/shard_map/all_to_all | solution.py:61
  36.4 104.3 %all-reduce.2.cloned.1.call-start = ((), (), s32[]{:S(2)}) async-start(), calls=%async_computation.3 | async-start | bytes 458752 | tf_op jit(solution)/shard_map/psum | solution.py:75
  50.9 188.6 %reduce-scatter.4.cloned.1.call-start = ((), (), s32[]{:S(2)}) async-start(), calls=%async_computation.4 | async-start | bytes 3899392
  141.8 0.7 copy-start.2
  151.1 90.8 %copy-start.1 = (bf16[8,384,576]{1,2,0:T(8,128)(2,1)S(1)}, bf16[8,384,576]{1,2,0:T(8,128)(2,1)}, u32[]{:S(2)}) copy-start(bf16[8,384,576]{1,2,0:T(8,128)(2,1)} %param.15) | copy-start | bytes 10616836
Sparse Core Ops, SparseCore 0:
  51.0 89.6 all-reduce.1
  169.9 69.5 reduce-scatter.3
where the time goes:
time: 249 us
  waiting for transfers between devices  166 us (67%)
  matrix products  40 us (16%)
  between operations  13.5 us (5%)
  blocking collectives  12.6 us (5%)
  starting transfers between devices  6.74 us (3%)
  local copies, waits for them, and re-layouts  5.54 us (2%)
  other arithmetic  4.23 us (2%)
    psum x1, waiting for transfers between devices, per_device(): attn_whole = lax.psum(attention, ('kvp', 'tp'))  89.8 us
    unnamed x3, waiting for transfers between devices  69.7 us
    unnamed x1, matrix products  18.6 us
    dot_general x1, matrix products, per_device(): gate_proj = jnp.dot(normed, w_gate, preferred_element_type=jnp.float32)  8.58 us
    dot_general x1, matrix products, project(): jnp.dot(head_out.reshape(head_out.shape[0], -1), w_out, preferred_element...  8.36 us
    all_gather x1, blocking collectives, per_device(): lax.all_gather(queries_rope, 'kvp', axis=1, tiled=True)  6.3 us
    all_gather x1, blocking collectives, per_device(): lax.all_gather(q_lat, 'kvp', axis=1, tiled=True)  6.27 us
    all_to_all x1, waiting for transfers between devices, per_device(): lax.all_to_all(blocks.astype(jnp.bfloat16), 'kvp', split_axis=1, concat_a...  5.84 us
  transfers between devices with their start and end apart: 4, of which 4 were waited for; matrix products, arithmetic and copies ran while one was open for 1% of the time, Pallas kernels for 0%

commit v1 on v0

--- a/solution.py
+++ b/solution.py
@@ -2,6 +2,11 @@
 import jax.numpy as jnp
 from jax import lax
 from jax.sharding import PartitionSpec as P
+
+
+def add_all(block, name):
+    parts = lax.all_gather(block, name)
+    return jnp.sum(parts, axis=0)
 
 
 def project(o_lat, w_uv, w_out):
@@ -72,7 +77,7 @@
     model_width = norm_gain.shape[0]
     share_width = model_width // lax.axis_size(("kvp", "tp"))
     share_start = lax.axis_index(("kvp", "tp")) * share_width
-    attn_whole = lax.psum(attention, ("kvp", "tp"))
+    attn_whole = add_all(attention, ("kvp", "tp"))
     residual = hidden_in.astype(jnp.float32) + attn_whole
     mean_square = jnp.mean(residual * residual, axis=1)
     normed = (residual * lax.rsqrt(mean_square + 1e-06)[:, None] * norm_gain[None, :]).astype(

time: 249 us -> 207 us (0.83)
  waiting for transfers between devices: 166 us -> 122 us
    psum x1 -> x0, waiting for transfers between devices: 89.8 us -> none  [per_device(): attn_whole = lax.psum(attention, ('kvp', 'tp'))]
    all_gather x0 -> x1, waiting for transfers between devices: none -> 48.2 us  [add_all(): parts = lax.all_gather(block, name)]
where the time goes in v1:
time: 207 us; the launch traced here: 206 us
  waiting for transfers between devices  122 us (59%)
  matrix products  40 us (19%)
  between operations  13.5 us (7%)
  blocking collectives  12.6 us (6%)
  starting transfers between devices  6.74 us (3%)
  local copies, waits for them, and re-layouts  5.54 us (3%)
  other arithmetic  5.52 us (3%)
    unnamed x3, waiting for transfers between devices  67.6 us
    all_gather x1, waiting for transfers between devices, add_all(): parts = lax.all_gather(block, name)  48.2 us
    unnamed x1, matrix products  18.6 us
    dot_general x1, matrix products, per_device(): gate_proj = jnp.dot(normed, w_gate, preferred_element_type=jnp.float32)  8.58 us
    dot_general x1, matrix products, project(): jnp.dot(head_out.reshape(head_out.shape[0], -1), w_out, preferred_element...  8.35 us
    all_gather x1, blocking collectives, per_device(): lax.all_gather(queries_rope, 'kvp', axis=1, tiled=True)  6.3 us
    all_gather x1, blocking collectives, per_device(): lax.all_gather(q_lat, 'kvp', axis=1, tiled=True)  6.27 us
    all_to_all x1, waiting for transfers between devices, per_device(): lax.all_to_all(blocks.astype(jnp.bfloat16), 'kvp', split_axis=1, concat_a...  5.84 us
  transfers between devices with their start and end apart: 4, of which 4 were waited for; matrix products, arithmetic and copies ran while one was open for 1% of the time, Pallas kernels for 0%

profile of v1, /device:TPU:0, one launch (start us, length us, event | category | flops | bytes accessed | tf_op | source)
XLA Modules:
  0.0 206.3 jit_solution(16578285809508608998)
XLA Ops:
  6.5 0.9 copy.24
  7.4 6.3 %all_gather.13 = bf16[8,32,64]{2,0,1:T(8,128)(2,1)S(1)} all-gather(bf16[8,8,64]{2,0,1:T(8,128)(2,1)S(1)} %copy.24), channel_id=1, replica_groups=mesh['grp'=2,'kvp'=4,'tp'=4] {'kvp'}, dimensions={1}, use_global_device_ids=true | all-gather | bytes 40960 | tf_op jit(solution)/shard_map/all_gather | solution.py:45
  13.7 1.5 fusion.2
  15.2 6.3 %all_gather.12 = bf16[8,32,512]{2,0,1:T(8,128)(2,1)S(1)} all-gather(bf16[8,8,512]{2,0,1:T(8,128)(2,1)S(1)} %fusion.2), channel_id=1, replica_groups=mesh['grp'=2,'kvp'=4,'tp'=4] {'kvp'}, dimensions={1}, use_global_device_ids=true | all-gather | bytes 327680 | tf_op jit(solution)/shard_map/all_gather | solution.py:44
  21.6 0.7 broadcast_compare_fusion
  22.3 0.7 fusion.31
  23.0 0.7 copy-done.3
  24.6 0.8 convert_element_type.50
  25.3 0.6 copy.27
  25.9 3.2 %all-to-all-start = ((bf16[8,4,8]{2,0,1:T(8,128)(2,1)}), bf16[8,4,8]{2,0,1:T(8,128)(2,1)S(1)}, u32[]{:S(2)}, u32[]{:S(2)}) async-start(bf16[8,4,8]{2,0,1:T(8,128)(2,1)} %copy.27), calls=%async_computation | async-start | bytes 16384 | tf_op jit(solution)/shard_map/all_to_all | solution.py:69
  29.2 2.2 %fusion.10 = bf16[8,32,576]{2,1,0:T(8,128)(2,1)S(1)} fusion(bf16[8,384,576]{1,2,0:T(8,128)(2,1)S(1)} %copy-done, f32[8,32,384]{2,1,0:T(8,128)} %copy-done.3, f32[8,32]{1,0:T(8,128)} %get-tuple-element.8, f32[8,32]{1,0:T(8,128)S(1)} %get-tuple-element.9, pred[8,384]{1,0:T(8,128)(4,1)S(1)} %broadcast_compare_fusion), kind=kOutput, calls=%fused_computation.23 | convolution fusion | flops 113639424 | bytes 4232192 | tf_op jit(solution)/shard_map/bht,btc->bhc/dot_general | solution.py:61
  31.5 0.7 copy.28
  32.2 0.8 all-to-all-done
  33.0 3.4 %all-to-all-start.1 = ((bf16[8,4,8,512]{3,2,0,1:T(8,128)(2,1)}), bf16[8,4,8,512]{3,2,0,1:T(8,128)(2,1)S(1)}, u32[]{:S(2)}, u32[]{:S(2)}) async-start(bf16[8,4,8,512]{3,2,0,1:T(8,128)(2,1)} %copy.28), calls=%async_computation.1 | async-start | bytes 524288 | tf_op jit(solution)/shard_map/all_to_all | solution.py:66
  36.5 5.8 %all-to-all-done.1 = bf16[8,4,8,512]{3,2,0,1:T(8,128)(2,1)S(1)} async-done(((bf16[8,4,8,512]{3,2,0,1:T(8,128)(2,1)}), bf16[8,4,8,512]{3,2,0,1:T(8,128)(2,1)S(1)}, u32[]{:S(2)}, u32[]{:S(2)}) %all-to-all-start.1) | async-done | bytes 262176 | tf_op jit(solution)/shard_map/all_to_all | solution.py:66
  42.5 8.3 %fusion.4 = f32[8,7168]{1,0:T(8,128)} fusion(bf16[1024,7168]{1,0:T(8,128)(2,1)} %param.19, bf16[8,512,128]{2,1,0:T(8,128)(2,1)} %param.18, bf16[8,8,512]{2,1,0:T(8,128)(2,1)S(1)} %multiply_reduce_fusion), kind=kOutput, calls=%fused_computation.10 | convolution fusion | flops 125837312 | bytes 16023552 | tf_op jit(solution)/shard_map/dot_general | solution.py:16
  50.9 48.2 %all-gather.3.cloned.1.call-done = f32[128,7168]{1,0:T(8,128)} async-done(((f32[8,7168]{1,0:T(8,128)}), f32[128,7168]{1,0:T(8,128)}) %all-gather.3.cloned.1.call-update) | async-done | bytes 3670032 | tf_op jit(solution)/shard_map/all_gather | solution.py:8
  99.1 2.2 %bitcast_reduce_fusion = f32[8,7168]{1,0:T(8,128)S(1)} fusion(f32[128,7168]{1,0:T(8,128)} %all-gather.3.cloned.1.call-done), kind=kLoop, calls=%fused_computation.1 | loop fusion | flops 860160 | bytes 3899392 | tf_op jit(solution)/shard_map/reduce_sum | solution.py:9
  101.5 0.7 copy-done.2
  102.2 8.6 %fusion.30 = f32[8,1152]{1,0:T(8,128)} fusion(bf16[7168,1152]{1,0:T(8,128)(2,1)} %param.21, f32[8,7168]{1,0:T(8,128)S(1)} %get-tuple-element.6, f32[7168]{0:T(1024)S(1)} %copy-done.4, f32[8]{0:T(128)S(1)} %add_rsqrt_fusion), kind=kOutput, calls=%fused_computation.51 | convolution fusion | flops 132292608 | bytes 16810016 | tf_op jit(solution)/shard_map/dot_general | solution.py:87
  110.8 18.6 %convolution_bitcast_fusion = f32[7168,8]{1,0:T(8,128)} fusion(bf16[1152,7168]{1,0:T(8,128)(2,1)} %param.23, bf16[7168,1152]{1,0:T(8,128)(2,1)} %param.22, f32[8,1152]{1,0:T(8,128)} %fusion.30, f32[8,7168]{1,0:T(8,128)} %copy-done.2, f32[7168]{0:T(1024)} %param.20, f32[8]{0:T(128)S(1)} %add_rsqrt_fusion), kind=kOutput, calls=%fused_computation | convolution fusion | flops 264468480 | bytes 33554464
  129.5 67.6 %reduce-scatter.4.cloned.1.call-done = f32[448,8]{1,0:T(8,128)} async-done(((f32[7168,8]{1,0:T(8,128)}), f32[448,8]{1,0:T(8,128)}) %reduce-scatter.4.cloned.1.call-update) | async-done | bytes 14352
  197.0 1.0 copy.32
  198.0 1.4 add_convert_fusion
  (28 shorter events, 1.4 us)
Async XLA Ops:
  6.5 15.7 %copy-start = (bf16[8,384,576]{1,2,0:T(8,128)(2,1)S(1)}, bf16[8,384,576]{1,2,0:T(8,128)(2,1)}, u32[]{:S(2)}) copy-start(bf16[8,384,576]{1,2,0:T(8,128)(2,1)} %param.15) | copy-start | bytes 10616836
  23.0 0.7 copy-start.3
  25.9 7.0 %all-to-all-start = ((bf16[8,4,8]{2,0,1:T(8,128)(2,1)}), bf16[8,4,8]{2,0,1:T(8,128)(2,1)S(1)}, u32[]{:S(2)}, u32[]{:S(2)}) async-start(bf16[8,4,8]{2,0,1:T(8,128)(2,1)} %copy.27), calls=%async_computation | async-start | bytes 16384 | tf_op jit(solution)/shard_map/all_to_all | solution.py:69
  31.4 69.9 %copy-start.5 = (bf16[8,7168]{1,0:T(8,128)(2,1)S(1)}, bf16[8,7168]{1,0:T(8,128)(2,1)}, u32[]{:S(2)}) copy-start(bf16[8,7168]{1,0:T(8,128)(2,1)} %param.12) | copy-start | bytes 344068
  31.5 70.8 %copy-start.4 = (f32[7168]{0:T(1024)S(1)}, f32[7168]{0:T(1024)}, u32[]{:S(2)}) copy-start(f32[7168]{0:T(1024)} %param.20) | copy-start | bytes 86020
  33.0 9.4 %all-to-all-start.1 = ((bf16[8,4,8,512]{3,2,0,1:T(8,128)(2,1)}), bf16[8,4,8,512]{3,2,0,1:T(8,128)(2,1)S(1)}, u32[]{:S(2)}, u32[]{:S(2)}) async-start(bf16[8,4,8,512]{3,2,0,1:T(8,128)(2,1)} %copy.28), calls=%async_computation.1 | async-start | bytes 524288 | tf_op jit(solution)/shard_map/all_to_all | solution.py:66
  36.4 62.7 %all-gather.3.cloned.1.call-start = ((), (), s32[]{:S(2)}) async-start(), calls=%async_computation.3 | async-start | bytes 3899392 | tf_op jit(solution)/shard_map/all_gather | solution.py:8
  50.9 146.2 %reduce-scatter.4.cloned.1.call-start = ((), (), s32[]{:S(2)}) async-start(), calls=%async_computation.4 | async-start | bytes 3899392
  101.5 0.7 copy-start.2
  110.8 88.7 %copy-start.1 = (bf16[8,384,576]{1,2,0:T(8,128)(2,1)S(1)}, bf16[8,384,576]{1,2,0:T(8,128)(2,1)}, u32[]{:S(2)}) copy-start(bf16[8,384,576]{1,2,0:T(8,128)(2,1)} %param.15) | copy-start | bytes 10616836
Sparse Core Ops, SparseCore 0:
  51.0 48.0 all-gather.2
  129.6 67.3 reduce-scatter.3
